TPU v7x, 256 devices: a whole 4x4x8 slice. The times are simulated.
256 devices in a mesh: dp: 16 (over y, x), row: 16 (over z, core).
Axes of the slice: x: 4, y: 4, z: 8, core: 2. Of those that a mesh axis runs over, the one named last changes fastest.
Arguments:
- bag_index: int32 [131072, 16], P(('dp', 'row')), may hold values from 0 to 9215, as said below
- pooled_grad: bfloat16 [131072, 256], P(('dp', 'row')), may hold values from -6 to 6
- touched_ids: int32 [256, 1024], P(('dp', 'row')), may hold values from 0 to 1023, as said below
- owner_counts: int32 [256, 256], P(('dp', 'row')), may hold values from 1 to 8, as said below
- cold_table: float32 [262144, 256], P(('dp', 'row')), may hold values from -6 to 6
- cold_moment_codes: bfloat16 [262144, 256], P(('dp', 'row')), may hold values from -1 to 1
- cold_second_codes: bfloat16 [262144, 256], P(('dp', 'row')), may hold values from 0.049804688 to 1
- cold_moment_scales: float32 [262144], P(('dp', 'row')), may hold values from 0.05 to 2
- cold_second_scales: float32 [262144], P(('dp', 'row')), may hold values from 0.01 to 1
- hot_table: float32 [8192, 256], replicated, may hold values from -6 to 6
- hot_moment_codes: bfloat16 [8192, 256], P('row'), may hold values from -1 to 1
- hot_second_codes: bfloat16 [8192, 256], P('row'), may hold values from 0.049804688 to 1
- hot_moment_scales: float32 [8192], P('row'), may hold values from 0.05 to 2
- hot_second_scales: float32 [8192], P('row'), may hold values from 0.01 to 1
Outputs:
- cold_table_new: float32 [262144, 256], P(('dp', 'row'))
- cold_moment_codes_new: bfloat16 [262144, 256], P(('dp', 'row'))
- cold_second_codes_new: bfloat16 [262144, 256], P(('dp', 'row'))
- cold_moment_scales_new: float32 [262144], P(('dp', 'row'))
- cold_second_scales_new: float32 [262144], P(('dp', 'row'))
- hot_replica: float32 [8192, 256], replicated
- hot_moment_codes_new: bfloat16 [8192, 256], P('row')
- hot_second_codes_new: bfloat16 [8192, 256], P('row')
- hot_moment_scales_new: float32 [8192], P('row')
- hot_second_scales_new: float32 [8192], P('row')
Inputs may be any that keep to these rules, and one draw needn't show every extreme that they name: `bag_index`: each device's rows of samples name every value below 1024 at least once; a value v of 1024 or more names hot row v - 1024. `owner_counts`: row k belongs to device k; its entries, one for each owning device in order along dp then row, sum to 1024; some owner gets 8 from every device. `touched_ids`: row k lists device k's touched rows grouped by owner in owner order, owner o's group holding owner_counts[k, o] entries; entries within a group are distinct.
All inputs are finite; a program needn't handle non-finite values.
Results may differ from a plain program's by a relative error of at most 0.001.
Values may be sent and summed in bfloat16 or wider, within the bound.
A program may use at most 128 MiB of HBM per device.

v0:
```python
import math

import jax
import jax.numpy as jnp
from jax import lax
from jax.sharding import PartitionSpec as P

CAP = 8


beta_one = 0.9
beta_two = 0.999
learn_rate = 0.1
adam_eps = 1e-08
bias_one = 1.0 - 1.7478712517226947e-46
bias_two = 0.6323045752290363


def split_up(array, dim, count):
    before, after = (array.shape[:dim], array.shape[dim + 1 :])
    return jnp.moveaxis(array.reshape(*before, count, -1, *after), dim, 0)


def in_order(tiles, dim):
    tiles = jnp.moveaxis(tiles, 0, dim)
    lengths = tiles.shape
    return tiles.reshape(*lengths[:dim], lengths[dim] * lengths[dim + 1], *lengths[dim + 2 :])


def one_exchange(array, axis, axes, splits, concats):
    sizes = [lax.axis_size(a) for a in axes]
    tiles = split_up(array, splits[0], sizes[0])
    tiles = jnp.moveaxis(split_up(tiles, splits[1] + 1, sizes[1]), 0, 1)
    inside = tiles.shape[2:]
    tiles = tiles.reshape(-1, *inside)
    tiles = lax.all_to_all(tiles, axis, split_axis=0, concat_axis=0, tiled=True)
    tiles = in_order(tiles.reshape(*sizes, *inside), concats[0] + 1)
    return in_order(tiles, concats[1])


def summed_on_arrival(array, axis, dim):
    count = lax.axis_size(axis)
    tiles = lax.all_to_all(split_up(array, dim, count), axis, 0, 0, tiled=True)
    return jnp.sum(tiles, axis=0)


def sent_together(arrays, axis, dim, along):
    widths = [math.prod(a.shape[along:]) for a in arrays]
    both = jnp.concatenate(
        [a.reshape(*a.shape[:along], w) for a, w in zip(arrays, widths)], axis=along
    )
    whole = lax.all_gather(both, axis, axis=dim, tiled=True)
    tiles = jnp.split(whole, [sum(widths[:k]) for k in range(1, len(widths))], axis=along)
    return tuple((b.reshape(*whole.shape[:along], *a.shape[along:]) for a, b in zip(arrays, tiles)))


def in_one_piece(arrays, axis, dim, along):
    both = jnp.concatenate(arrays, axis=along)
    whole, at, done = (lax.all_gather(both, axis, axis=dim, tiled=True), 0, [])
    for a in arrays:
        done.append(lax.slice_in_dim(whole, at, at + a.shape[along], axis=along))
        at += a.shape[along]
    return tuple(done)


def adam_rows(weights, moment_codes, second_codes, moment_scales, second_scales, gradient):
    moment = (
        beta_one * moment_scales[:, None] * moment_codes.astype(jnp.float32)
        + (1.0 - beta_one) * gradient
    )
    second = (
        beta_two * second_scales[:, None] * second_codes.astype(jnp.float32)
        + (1.0 - beta_two) * gradient * gradient
    )
    updated = weights - learn_rate * (moment / bias_one) / (jnp.sqrt(second / bias_two) + adam_eps)
    moment_scale_new = jnp.max(jnp.abs(moment), axis=1) + 1e-06
    second_scale_new = jnp.max(second, axis=1) + 1e-06
    moment_code_new = (moment / moment_scale_new[:, None]).astype(jnp.bfloat16)
    second_code_new = (second / second_scale_new[:, None]).astype(jnp.bfloat16)
    return (updated, moment_code_new, second_code_new, moment_scale_new, second_scale_new)


def take_rows(array, first_row, row_count):
    return lax.dynamic_slice_in_dim(array, first_row, row_count, 0)


def body(
    bag_index,
    pooled_grad,
    touched_ids,
    owner_counts,
    cold_table,
    cold_moment_codes,
    cold_second_codes,
    cold_moment_scales,
    cold_second_scales,
    hot_table,
    hot_moment_codes,
    hot_second_codes,
    hot_moment_scales,
    hot_second_scales,
):
    dp_size = lax.axis_size("dp")
    row_size = lax.axis_size("row")
    touch_rows = touched_ids.shape[1]
    hot_rows = hot_table.shape[0]
    local_rows = touch_rows + hot_rows
    features = pooled_grad.shape[1]
    block_rows = math.gcd(local_rows, 512)

    def tally_block(first_column):
        columns = first_column + lax.iota(jnp.int32, block_rows)
        tally = jnp.sum(
            (bag_index[:, :, None] == columns[None, None, :]).astype(jnp.bfloat16), axis=1
        )
        return lax.dot_general(
            tally, pooled_grad, (((0,), (0,)), ((), ())), preferred_element_type=jnp.float32
        )

    starts_list = jnp.arange(local_rows // block_rows, dtype=jnp.int32) * block_rows
    gradient = lax.map(tally_block, starts_list).reshape(local_rows, features)
    count_row = owner_counts[0]
    run_start = jnp.cumsum(count_row) - count_row
    slot_index = lax.iota(jnp.int32, CAP)
    is_live = slot_index[None, :] < count_row[:, None]
    position = jnp.where(is_live, run_start[:, None] + slot_index[None, :], 0)
    bucket_grad = jnp.where(is_live[:, :, None], gradient[:touch_rows][position], 0.0).reshape(
        dp_size, row_size, CAP, features
    )
    bucket_ids = jnp.where(is_live, touched_ids[0][position], 0).reshape(dp_size, row_size, CAP)
    arrived, arrived_ids = (
        one_exchange(bucket_grad, ("dp", "row"), ("dp", "row"), (0, 1), (0, 1)),
        one_exchange(bucket_ids, ("dp", "row"), ("dp", "row"), (0, 1), (0, 1)),
    )
    owned_grad = jax.ops.segment_sum(
        arrived.reshape(-1, features), arrived_ids.reshape(-1), num_segments=cold_table.shape[0]
    )
    cold = adam_rows(
        cold_table,
        cold_moment_codes,
        cold_second_codes,
        cold_moment_scales,
        cold_second_scales,
        owned_grad,
    )
    hot_grad = gradient[touch_rows:]
    block_count = hot_moment_codes.shape[0]
    row_start = lax.axis_index("row") * block_count
    own_weights = take_rows(hot_table, row_start, block_count)
    block_grad = lax.psum_scatter(hot_grad, "row", scatter_dimension=0, tiled=True)
    shard_grad = summed_on_arrival(block_grad, "dp", 0)
    piece_rows = block_count // dp_size
    piece_start = lax.axis_index("dp") * piece_rows
    piece = adam_rows(
        take_rows(own_weights, piece_start, piece_rows),
        take_rows(hot_moment_codes, piece_start, piece_rows),
        take_rows(hot_second_codes, piece_start, piece_rows),
        take_rows(hot_moment_scales, piece_start, piece_rows),
        take_rows(hot_second_scales, piece_start, piece_rows),
        shard_grad,
    )
    weights_back, moment_scales_back, second_scales_back = sent_together(
        (piece[0], piece[3], piece[4]), "dp", 0, 1
    )
    moment_codes_back, second_codes_back = in_one_piece((piece[1], piece[2]), "dp", 0, 1)
    hot_new = (
        weights_back,
        moment_codes_back,
        second_codes_back,
        moment_scales_back,
        second_scales_back,
    )
    replica = lax.all_gather(hot_new[0], "row", axis=0, tiled=True)
    return (
        cold[0],
        cold[1],
        cold[2],
        cold[3],
        cold[4],
        replica,
        hot_new[1],
        hot_new[2],
        hot_new[3],
        hot_new[4],
    )


def solution(mesh):
    return jax.shard_map(
        body,
        mesh=mesh,
        in_specs=(
            P(("dp", "row"), None),
            P(("dp", "row"), None),
            P(("dp", "row"), None),
            P(("dp", "row"), None),
            P(("dp", "row"), None),
            P(("dp", "row"), None),
            P(("dp", "row"), None),
            P(("dp", "row")),
            P(("dp", "row")),
            P(),
            P("row", None),
            P("row", None),
            P("row"),
            P("row"),
        ),
        out_specs=(
            P(("dp", "row"), None),
            P(("dp", "row"), None),
            P(("dp", "row"), None),
            P(("dp", "row")),
            P(("dp", "row")),
            P(),
            P("row", None),
            P("row", None),
            P("row"),
            P("row"),
        ),
        check_vma=False,
    )
```

profile of v0, /device:TPU:1, one launch (start us, length us, event | category | flops | bytes accessed | tf_op | source)
XLA Modules:
  0.0 415.9 jit_solution(15215305488470885821)
XLA Ops:
  8.1 126.4 %while.12 = (s32[]{:T(128)}, f32[18,512,256]{2,1,0:T(8,128)}, s32[512,16]{1,0:T(8,128)S(1)}, s32[18]{0:T(128)S(1)}, bf16[512,256]{1,0:T(8,128)(2,1)}, /*index=5*/s32[]{:T(128)}) while((s32[]{:T(128)}, f32[18,512,256]{2,1,0:T(8,128)}, s32[512,16]{1,0:T(8,128)S(1)}, s32[18]{0:T(128)S(1)}, bf16[512,256]{1,0:T(8,128)(2,1)}, ...), condition=%wide.region_4.5_spmd, body=%wide.region_2.4_spmd.sunk | while | flops 146539008 | bytes 1871969 | solution.py:121
  9.4 3.7 fusion.21
  16.4 3.7 fusion.21
  23.4 3.7 fusion.21
  30.5 3.7 fusion.21
  37.5 3.7 fusion.21
  44.5 3.7 fusion.21
  51.5 3.7 fusion.21
  58.5 3.7 fusion.21
  65.5 3.7 fusion.21
  72.5 3.7 fusion.21
  79.6 3.7 fusion.21
  86.6 3.7 fusion.21
  93.6 3.7 fusion.21
  100.6 3.7 fusion.21
  107.7 3.7 fusion.21
  128.7 3.7 fusion.21
  134.6 7.5 %slice.29 = f32[16,512,256]{2,1,0:T(8,128)} slice(f32[18,512,256]{2,1,0:T(8,128)} %get-tuple-element.75), slice={[2:18], [0:512], [0:256]} | slice | bytes 16777216 | tf_op jit(solution)/shard_map/slice | solution.py:146
  142.1 71.7 %reduce-scatter.2.cloned.1.call-done = f32[512,256]{1,0:T(8,128)} async-done(((f32[8192,256]{1,0:T(8,128)}), f32[512,256]{1,0:T(8,128)}) %reduce-scatter.2.cloned.1.call-update) | async-done | bytes 524304 | tf_op jit(solution)/shard_map/reduce_scatter | solution.py:150
  213.8 6.7 %all-to-all-start.2 = ((f32[16,32,256]{2,1,0:T(8,128)}), f32[16,32,256]{2,1,0:T(8,128)S(1)}, u32[]{:S(2)}, u32[]{:S(2)}) async-start(f32[16,32,256]{2,1,0:T(8,128)} %bitcast.59), calls=%async_computation.3 | async-start | bytes 1048576 | tf_op jit(solution)/shard_map/all_to_all | solution.py:43
  221.4 8.4 %all-to-all-done.2 = f32[16,32,256]{2,1,0:T(8,128)S(1)} async-done(((f32[16,32,256]{2,1,0:T(8,128)}), f32[16,32,256]{2,1,0:T(8,128)S(1)}, u32[]{:S(2)}, u32[]{:S(2)}) %all-to-all-start.2) | async-done | bytes 524320 | tf_op jit(solution)/shard_map/all_to_all | solution.py:43
  231.2 16.9 %all_gather.9 = f32[512,258]{1,0:T(8,128)S(1)} all-gather(f32[32,258]{1,0:T(8,128)S(1)} %pad_maximum_fusion), channel_id=1, replica_groups=mesh['dp'=16,'row'=16] {'dp'}, dimensions={0}, use_global_device_ids=true | all-gather | bytes 561408 | tf_op jit(solution)/shard_map/all_gather | solution.py:52
  250.7 8.6 %gather_fusion = s32[2048]{0:T(1024)S(1)} fusion(s32[1024]{0:T(1024)S(1)} %bitcast.56, s32[2048]{0:T(1024)S(1)} %broadcast_clamp_fusion), kind=kCustom, calls=%fused_computation | custom fusion | bytes 24576 | tf_op jit(solution)/shard_map/gather | solution.py:130
  260.2 18.2 %all-to-all-start = ((s32[256,1,1,8]{3,2,1,0:T(1,128)}), s32[256,1,1,8]{3,2,1,0:T(1,128)S(1)}, u32[]{:S(2)}, u32[]{:S(2)}) async-start(s32[256,1,1,8]{3,2,1,0:T(1,128)} %bitcast.6), calls=%async_computation | async-start | bytes 262144 | tf_op jit(solution)/shard_map/all_to_all | solution.py:36
  279.8 6.6 %gather_fusion.1 = f32[2048,256]{1,0:T(8,128)S(1)} fusion(f32[1024,256]{1,0:T(8,128)S(1)} %bitcast.57, s32[2048]{0:T(1024)S(1)} %broadcast_clamp_fusion), kind=kCustom, calls=%fused_computation.1 | custom fusion | bytes 4202496 | tf_op jit(solution)/shard_map/gather | solution.py:127
  288.2 4.8 %all-to-all-done = s32[256,1,1,8]{3,2,1,0:T(1,128)S(1)} async-done(((s32[256,1,1,8]{3,2,1,0:T(1,128)}), s32[256,1,1,8]{3,2,1,0:T(1,128)S(1)}, u32[]{:S(2)}, u32[]{:S(2)}) %all-to-all-start) | async-done | bytes 8224 | tf_op jit(solution)/shard_map/all_to_all | solution.py:36
  293.0 8.9 %all-to-all-start.1 = ((f32[256,1,1,8,256]{4,3,2,1,0:T(8,128)}), f32[256,1,1,8,256]{4,3,2,1,0:T(8,128)S(1)}, u32[]{:S(2)}, u32[]{:S(2)}) async-start(f32[256,1,1,8,256]{4,3,2,1,0:T(8,128)} %bitcast_select_fusion), calls=%async_computation.1 | async-start | bytes 4194304 | tf_op jit(solution)/shard_map/all_to_all | solution.py:36
  302.1 63.1 %all-to-all-done.1 = f32[256,1,1,8,256]{4,3,2,1,0:T(8,128)S(1)} async-done(((f32[256,1,1,8,256]{4,3,2,1,0:T(8,128)}), f32[256,1,1,8,256]{4,3,2,1,0:T(8,128)S(1)}, u32[]{:S(2)}, u32[]{:S(2)}) %all-to-all-start.1) | async-done | bytes 2097184 | tf_op jit(solution)/shard_map/all_to_all | solution.py:36
  365.1 11.9 %scatter_custom_fusion = f32[1024,256]{1,0:T(8,128)S(1)} fusion(s32[2048]{0:T(1024)S(1)} %reshape.287, f32[256,1,1,8,256]{4,3,2,1,0:T(8,128)S(1)} %all-to-all-done.1, f32[]{:T(128)} %constant.68.clone.1), kind=kCustom, calls=%fused_computation.8 | custom fusion | flops 524288 | bytes 3145732 | tf_op jit(solution)/shard_map/scatter-add | solution.py:135
  377.1 3.7 fusion.11
  383.3 16.8 %all_gather.11 = bf16[512,512]{1,0:T(8,128)(2,1)S(1)} all-gather(bf16[32,512]{1,0:T(8,128)(2,1)S(1)} %pad_maximum_fusion.1), channel_id=1, replica_groups=mesh['dp'=16,'row'=16] {'dp'}, dimensions={0}, use_global_device_ids=true | all-gather | bytes 557056 | tf_op jit(solution)/shard_map/all_gather | solution.py:59
  401.8 7.3 %copy.48 = f32[8192,256]{1,0:T(8,128)} copy(f32[8192,256]{1,0:T(8,128)} %all-gather.2.cloned.1.call-done) | data formatting | bytes 16777216
  (115 shorter events, 81.5 us)
Async XLA Ops:
  7.2 243.5 %copy-start = (s32[1,1024]{1,0:T(1,128)S(1)}, s32[1,1024]{1,0:T(1,128)}, u32[]{:S(2)}) copy-start(s32[1,1024]{1,0:T(1,128)} %param.18) | copy-start | bytes 12292
  7.2 206.6 %reduce-scatter.2.cloned.1.call-start = ((), (), s32[]{:S(2)}) async-start(), calls=%async_computation.4 | async-start | bytes 8912896 | tf_op jit(solution)/shard_map/reduce_scatter | solution.py:150
  142.1 107.7 %copy-start.5 = (s32[1,256]{1,0:T(1,128)S(1)}, s32[1,256]{1,0:T(1,128)}, u32[]{:S(2)}) copy-start(s32[1,256]{1,0:T(1,128)} %param.19) | copy-start | bytes 3076
  213.8 16.0 %all-to-all-start.2 = ((f32[16,32,256]{2,1,0:T(8,128)}), f32[16,32,256]{2,1,0:T(8,128)S(1)}, u32[]{:S(2)}, u32[]{:S(2)}) async-start(f32[16,32,256]{2,1,0:T(8,128)} %bitcast.59), calls=%async_computation.3 | async-start | bytes 1048576 | tf_op jit(solution)/shard_map/all_to_all | solution.py:43
  220.6 181.2 %all-gather.2.cloned.1.call-start = ((), (), s32[]{:S(2)}) async-start(), calls=%async_computation.5 | async-start | bytes 8912896 | tf_op jit(solution)/shard_map/all_gather | solution.py:173
  248.0 0.9 copy-start.1
  260.2 32.8 %all-to-all-start = ((s32[256,1,1,8]{3,2,1,0:T(1,128)}), s32[256,1,1,8]{3,2,1,0:T(1,128)S(1)}, u32[]{:S(2)}, u32[]{:S(2)}) async-start(s32[256,1,1,8]{3,2,1,0:T(1,128)} %bitcast.6), calls=%async_computation | async-start | bytes 262144 | tf_op jit(solution)/shard_map/all_to_all | solution.py:36
  286.5 15.4 %copy-start.8 = (f32[1024]{0:T(1024)S(1)}, f32[1024]{0:T(1024)}, u32[]{:S(2)}) copy-start(f32[1024]{0:T(1024)} %param.23) | copy-start | bytes 12292
  286.5 15.4 %copy-start.9 = (f32[1024]{0:T(1024)S(1)}, f32[1024]{0:T(1024)}, u32[]{:S(2)}) copy-start(f32[1024]{0:T(1024)} %param.24) | copy-start | bytes 12292
  293.0 72.2 %all-to-all-start.1 = ((f32[256,1,1,8,256]{4,3,2,1,0:T(8,128)}), f32[256,1,1,8,256]{4,3,2,1,0:T(8,128)S(1)}, u32[]{:S(2)}, u32[]{:S(2)}) async-start(f32[256,1,1,8,256]{4,3,2,1,0:T(8,128)} %bitcast_select_fusion), calls=%async_computation.1 | async-start | bytes 4194304 | tf_op jit(solution)/shard_map/all_to_all | solution.py:36
  377.0 3.7 copy-start.3
  377.0 3.7 copy-start.4
  377.1 23.0 %copy-start.2 = (f32[512,258]{1,0:T(8,128)S(1)}, f32[512,258]{1,0:T(8,128)}, u32[]{:S(2)}) copy-start(f32[512,258]{1,0:T(8,128)} %copy-done.1) | copy-start | bytes 1585156
  380.7 28.4 %copy-start.6 = (f32[1024]{0:T(1024)}, f32[1024]{0:T(1024)S(1)}, u32[]{:S(2)}) copy-start(f32[1024]{0:T(1024)S(1)} %get-tuple-element.176) | copy-start | bytes 12292
  380.7 28.4 %copy-start.7 = (f32[1024]{0:T(1024)}, f32[1024]{0:T(1024)S(1)}, u32[]{:S(2)}) copy-start(f32[1024]{0:T(1024)S(1)} %get-tuple-element.175) | copy-start | bytes 12292
Sparse Core Ops, SparseCore 0:
  142.3 71.5 reduce-scatter.1
  249.9 85.2 all-gather.1
where the time goes:
time: 420 us; the launch traced here: 416 us
  waiting for transfers between devices  148 us (35%)
  other arithmetic  101 us (24%)
  local copies, waits for them, and re-layouts  47 us (11%)
  matrix products  37.9 us (9%)
  starting transfers between devices  33.9 us (8%)
  blocking collectives  33.7 us (8%)
  between operations  14.3 us (3%)
    reduce_scatter x1, waiting for transfers between devices, body(): lax.psum_scatter(hot_grad, 'row', scatter_dimension=0, tiled=True)  71.7 us
    all_to_all x2, waiting for transfers between devices, one_exchange(): tiles = lax.all_to_all(tiles, axis, split_axis=0, concat_axis=0, tiled=True)  67.8 us
    reduce_sum x18, other arithmetic, tally_block(): jnp.sum((bag_index[:, :, None] == columns[None, None, :]).astype(jnp.bflo...  66.1 us
    dot_general x18, matrix products, tally_block(): lax.dot_general(tally, pooled_grad, (((0,), (0,)), ((), ())), preferred_e...  37.9 us
    all_to_all x2, starting transfers between devices, one_exchange(): tiles = lax.all_to_all(tiles, axis, split_axis=0, concat_axis=0, tiled=True)  27.1 us
    all_gather x1, blocking collectives, sent_together(): whole = lax.all_gather(both, axis, axis=dim, tiled=True)  16.9 us
    all_gather x1, blocking collectives, in_one_piece(): whole, at, done = (lax.all_gather(both, axis, axis=dim, tiled=True), 0, [])  16.8 us
    scatter-add x1, other arithmetic, body(): jax.ops.segment_sum(arrived.reshape(-1, features), arrived_ids.reshape(-1...  11.9 us
  transfers between devices with their start and end apart: 5, of which 4 were waited for; matrix products, arithmetic and copies ran while one was open for 10% of the time, Pallas kernels for 0%

commit v1 on v0

v1 whole, which is shorter than its diff:
```python
import functools

import jax
import jax.numpy as jnp
from jax import lax
from jax.experimental import pallas as pl
from jax.experimental.pallas import tpu as pltpu
from jax.sharding import PartitionSpec as P

CAP = 8
beta_one = 0.9
beta_two = 0.999
learn_rate = 0.1
adam_eps = 1e-08
bias_one = 1.0 - 1.7478712517226947e-46
bias_two = 0.6323045752290363

MESH = pl.DeviceIdType.MESH
F32 = jnp.float32
BF16 = jnp.bfloat16
I32 = jnp.int32
NIBBLES = 0x0F0F0F0F


def adam_parts(codes_m, codes_s, scale_m, scale_s, grad):
    moment = beta_one * scale_m * codes_m.astype(F32) + (1.0 - beta_one) * grad
    second = beta_two * scale_s * codes_s.astype(F32) + (1.0 - beta_two) * grad * grad
    update = learn_rate * (moment / bias_one) / (jnp.sqrt(second / bias_two) + adam_eps)
    new_m = jnp.max(jnp.abs(moment), axis=1, keepdims=True) + 1e-06
    new_s = jnp.max(second, axis=1, keepdims=True) + 1e-06
    return (
        update,
        (moment / new_m).astype(BF16),
        (second / new_s).astype(BF16),
        new_m,
        new_s,
    )


def lanes_to_column(line, rows, first):
    shape = (rows, line.shape[1])
    at = lax.broadcasted_iota(I32, shape, 1) == lax.broadcasted_iota(I32, shape, 0) + first
    return jnp.sum(jnp.where(at, jnp.broadcast_to(line, shape), 0.0), axis=1, keepdims=True)


def column_to_lanes(column, lanes):
    shape = (column.shape[0], lanes)
    at = lax.broadcasted_iota(I32, shape, 1) == lax.broadcasted_iota(I32, shape, 0)
    return jnp.sum(jnp.where(at, jnp.broadcast_to(column, shape), 0.0), axis=0, keepdims=True)


def exchange_kernel(
    n_dp,
    n_row,
    pool_ref,
    note_ref,
    codes_m_ref,
    codes_s_ref,
    scale_m_ref,
    scale_s_ref,
    cold_in,
    ids_in,
    steps_q,
    steps_scale,
    new_m_ref,
    new_s_ref,
    lines_ref,
    pools,
    notes,
    tally,
    hot_sum,
    cold_out,
    ids_out,
    hot_in,
    line_out,
    pool_sems,
    note_sems,
    step_sems,
    step_scale_sems,
    bulk_sems,
    local_sems,
):
    d = lax.axis_index("dp")
    r = lax.axis_index("row")
    chips = n_row // 2
    z, c = r // 2, r % 2
    sign = 1 - 2 * c
    half = pool_ref.shape[0] // 2
    block = hot_sum.shape[0]
    piece = block // n_dp
    slots = n_dp * CAP
    main_hops, other_hops = chips // 2, chips // 2 - 1

    def row_of(chip, core):
        return lax.rem(chip + 2 * chips, chips) * 2 + core

    main_to = row_of(z + sign, c)
    other_to = row_of(z - sign, c)
    sibling = row_of(z, 1 - c)

    def peer(i):
        return lax.rem(d + i, n_dp)

    own = pltpu.make_async_copy(pool_ref, pools.at[r], local_sems.at[0])
    own_note = pltpu.make_async_copy(note_ref, notes.at[r], local_sems.at[1])
    own.start()
    own_note.start()

    barrier = pltpu.get_barrier_semaphore()
    for to in (main_to, other_to, sibling):
        pl.semaphore_signal(barrier, inc=1, device_id=(d, to), device_id_type=MESH)

    def greet(i, carry):
        pl.semaphore_signal(barrier, inc=1, device_id=(peer(i), r), device_id_type=MESH)
        return carry

    lax.fori_loop(1, n_dp, greet, 0)
    own.wait()
    own_note.wait()
    hot_sum[...] = jnp.zeros_like(hot_sum)
    pl.semaphore_wait(barrier, n_dp + 2)

    def ring(big, small, big_sems, small_sems, use):
        span = big.shape[1] // 2

        def copies(source, b, to, lane, k):
            at = big.at[source, pl.ds(b * span, span)]
            n = k * 2 + b
            yield pltpu.make_async_remote_copy(
                src_ref=at,
                dst_ref=at,
                send_sem=big_sems.at[2 * lane, n],
                recv_sem=big_sems.at[2 * lane + 1, n],
                device_id=(d, to),
                device_id_type=MESH,
            )

        def note(source, to, lane, k):
            return pltpu.make_async_remote_copy(
                src_ref=small.at[source],
                dst_ref=small.at[source],
                send_sem=small_sems.at[2 * lane, k],
                recv_sem=small_sems.at[2 * lane + 1, k],
                device_id=(d, to),
                device_id_type=MESH,
            )

        def send(source, b, to, lane, k):
            if b == 0:
                note(source, to, lane, k).start()
            for copy in copies(source, b, to, lane, k):
                copy.start()

        def arrive(source, b, to, lane, k):
            if b == 0:
                note(source, to, lane, k).wait_recv()
            for copy in copies(source, b, to, lane, k):
                copy.wait_recv()

        def sent(source, b, to, lane, k):
            if b == 0:
                note(source, to, lane, k).wait_send()
            for copy in copies(source, b, to, lane, k):
                copy.wait_send()

        def step(k, carry):
            from_main = row_of(z - sign * k, c)
            from_other = row_of(z + sign * k, c)
            has_other = jnp.logical_and(k >= 1, k <= other_hops)
            for b in range(2):

                @pl.when(k >= 1)
                def _():
                    arrive(from_main, b, main_to, 0, k - 1)

                @pl.when(k < main_hops)
                def _():
                    send(from_main, b, main_to, 0, k)

                @pl.when(has_other)
                def _():
                    arrive(from_other, b, other_to, 1, k - 1)

                @pl.when(k < other_hops)
                def _():
                    send(from_other, b, other_to, 1, k)

                send(from_main, b, sibling, 2, k)

                @pl.when(has_other)
                def _():
                    send(from_other, b, sibling, 2, main_hops + k)

                if use is None:
                    continue

                def turn(q, inner):
                    live = jnp.logical_or(q % 2 == 0, has_other)

                    @pl.when(live)
                    def _():
                        there = jnp.where(
                            jnp.logical_or(q == 0, q == 3), from_main // 2, from_other // 2
                        )
                        source = there * 2 + jnp.where(q < 2, c, 1 - c)

                        @pl.when(q >= 2)
                        def _():
                            arrive(source, b, sibling, 2, k + jnp.where(q == 3, main_hops, 0))

                        use(source, b)

                    return inner

                lax.fori_loop(0, 4, turn, 0)
            return carry

        lax.fori_loop(0, main_hops + 1, step, 0)

        for k in range(main_hops):
            for b in range(2):
                sent(r, b, main_to, 0, k)
        for k in range(other_hops):
            for b in range(2):
                sent(r, b, other_to, 1, k)
        for k in range(main_hops + 1 + other_hops):
            for b in range(2):
                sent(r, b, sibling, 2, k)
                if use is None:
                    arrive(r, b, sibling, 2, k)

    rows_at = lax.broadcasted_iota(I32, (8, 128), 0)
    hot_first = n_row * slots + r * block
    cold_first = r * slots
    low = block // 8
    cold_low = slots // 8
    groups = low // 16

    def count(source, b):
        def tile(t, carry):
            first = pl.multiple_of(t * 128, 128)
            high, field = [], []
            for j in range(16):
                word = jnp.broadcast_to(notes[source, j : j + 1, pl.ds(first, 128)], (8, 128))
                value = word & 0xFFFF if b == 0 else lax.shift_right_logical(word, 16)
                hot = value - hot_first
                cold = value - cold_first
                is_hot = jnp.logical_and(hot >= 0, hot < block)
                is_cold = jnp.logical_and(cold >= 0, cold < slots)
                top = jnp.where(is_cold, cold // cold_low, lax.shift_right_logical(hot, low.bit_length() - 1) & 7)
                high.append(
                    jnp.where(is_cold, low + (cold & (cold_low - 1)), hot & (low - 1)) - rows_at
                )
                field.append(
                    jnp.where(
                        jnp.logical_or(is_hot, is_cold),
                        lax.shift_left(jnp.ones_like(top), (top & 7) * 4),
                        0,
                    )
                )
            for k in range(groups + 1):
                parts = []
                for h in range(2):
                    base = (k * 2 + h) * 8
                    sums = []
                    for g in range(2):
                        total = jnp.zeros((8, 128), I32)
                        for j in range(8 * g, 8 * g + 8):
                            total = total + jnp.where(high[j] == base, field[j], 0)
                        sums.append(total)
                    even = (sums[0] & NIBBLES) + (sums[1] & NIBBLES)
                    odd = (lax.shift_right_logical(sums[0], 4) & NIBBLES) + (
                        lax.shift_right_logical(sums[1], 4) & NIBBLES
                    )
                    parts.append((even, odd))
                for f in range(8):
                    found = []
                    for h in range(2):
                        x = lax.shift_right_logical(parts[h][f & 1], 8 * (f >> 1))
                        found.append((x & 255).astype(F32))
                    row = f * low + k * 16 if k < groups else block + f * 16
                    tally[pl.ds(row, 16), pl.ds(first, 128)] = jnp.concatenate(found, 0).astype(BF16)
            return carry

        lax.fori_loop(0, half // 128, tile, 0)
        rows = pools[source, pl.ds(b * half, half), :]
        hot_sum[...] += jnp.dot(tally[:block, :], rows, preferred_element_type=F32)
        cold = jnp.dot(tally[block:, :], rows, preferred_element_type=F32)
        if b == 0:
            cold_out[source] = cold
        else:
            cold_out[source] += cold
            cold_in[d, source] = cold_out[source, pl.ds(pl.multiple_of(d * CAP, CAP), CAP), :]
            held = notes[source, :, half:]
            wanted = lax.broadcasted_iota(I32, held.shape, 0) == r
            ids_out[source] = jnp.sum(jnp.where(wanted, held, 0), axis=0)

            def give(i, carry):
                to = peer(i)
                pltpu.make_async_remote_copy(
                    src_ref=cold_out.at[source, pl.ds(pl.multiple_of(to * CAP, CAP), CAP)],
                    dst_ref=cold_in.at[d, source],
                    send_sem=bulk_sems.at[0],
                    recv_sem=bulk_sems.at[1],
                    device_id=(to, r),
                    device_id_type=MESH,
                ).start()
                return carry

            lax.fori_loop(1, n_dp, give, 0)

    ring(pools, notes, pool_sems, note_sems, count)

    def to_all(make):
        def go(i, carry):
            make(peer(i)).start()
            return carry

        lax.fori_loop(1, n_dp, go, 0)

    def to_dp(src, dst, n):
        def make(to):
            return pltpu.make_async_remote_copy(
                src_ref=src(to),
                dst_ref=dst,
                send_sem=bulk_sems.at[n],
                recv_sem=bulk_sems.at[n + 1],
                device_id=(to, r),
                device_id_type=MESH,
            )

        return make

    def all_bytes(ref, n):
        return pltpu.make_async_remote_copy(
            src_ref=ref,
            dst_ref=ref,
            send_sem=bulk_sems.at[n],
            recv_sem=bulk_sems.at[n + 1],
            device_id=(peer(1), r),
            device_id_type=MESH,
        )

    others = pl.ds(0, n_dp - 1)
    to_all(
        to_dp(
            lambda to: hot_sum.at[pl.ds(pl.multiple_of(to * piece, piece), piece)], hot_in.at[d], 2
        )
    )
    ids_in[d] = ids_out[...]
    to_all(to_dp(lambda to: ids_out, ids_in.at[d], 4))
    mine = pl.ds(pl.multiple_of(d * piece, piece), piece)
    hot_in[d] = hot_sum[mine, :]
    all_bytes(hot_in.at[others], 2).wait_recv()
    grad = hot_in[0]
    for k in range(1, n_dp):
        grad = grad + hot_in[k]
    per_line = 128 // piece
    line_at = pl.ds(d // per_line, 1)
    first = lax.rem(d, per_line) * piece
    update, new_m, new_s, new_scale_m, new_scale_s = adam_parts(
        codes_m_ref[mine, :],
        codes_s_ref[mine, :],
        lanes_to_column(scale_m_ref[line_at, :], piece, first),
        lanes_to_column(scale_s_ref[line_at, :], piece, first),
        grad,
    )
    widest = jnp.maximum(jnp.max(jnp.abs(update), axis=1, keepdims=True), 1e-20)
    steps_q[r, mine, :] = jnp.round(update * (32767.0 / widest)).astype(I32).astype(jnp.int16)
    line_out[0:1, :] = column_to_lanes(new_scale_m, 128)
    line_out[1:2, :] = column_to_lanes(new_scale_s, 128)
    line_out[2:3, :] = column_to_lanes(widest / 32767.0, 128)
    line_out[3:8, :] = jnp.zeros((5, 128), F32)
    new_m_ref[mine, :] = new_m
    new_s_ref[mine, :] = new_s
    lines_ref[d] = line_out[...]
    to_all(to_dp(lambda to: line_out, lines_ref.at[d], 6))
    to_all(to_dp(lambda to: steps_q.at[r, mine], steps_q.at[r, mine], 8))
    to_all(to_dp(lambda to: new_m_ref.at[mine], new_m_ref.at[mine], 10))
    to_all(to_dp(lambda to: new_s_ref.at[mine], new_s_ref.at[mine], 12))
    all_bytes(lines_ref.at[others], 6).wait_recv()
    for k in range(n_dp):
        steps_scale[r, k : k + 1, :] = lines_ref[k, 2:3, :]
    rest = pl.ds(0, block - piece)
    all_bytes(steps_q.at[r, rest], 8).wait_recv()

    ring(steps_q, steps_scale, step_sems, step_scale_sems, None)

    for ref, n in (
        (cold_in.at[others], 0),
        (ids_in.at[others], 4),
        (new_m_ref.at[rest], 10),
        (new_s_ref.at[rest], 12),
    ):
        all_bytes(ref, n).wait()
    for ref, n in (
        (hot_in.at[others], 2),
        (lines_ref.at[others], 6),
        (steps_q.at[r, rest], 8),
    ):
        all_bytes(ref, n).wait_send()


def cold_kernel(
    values_ref,
    ids_ref,
    table_ref,
    codes_m_ref,
    codes_s_ref,
    scale_m_ref,
    scale_s_ref,
    table_out,
    codes_m_out,
    codes_s_out,
    scale_m_out,
    scale_s_out,
    split,
):
    n = pl.program_id(0)
    rows, width = table_ref.shape

    @pl.when(n == 0)
    def _():
        value = values_ref[...]
        top = value.astype(BF16)
        split[:, :width] = top
        split[:, width:] = (value - top.astype(F32)).astype(BF16)

    ids = ids_ref[...]
    shape = (rows, ids.shape[1])
    wanted = lax.broadcasted_iota(I32, shape, 0) + n * rows
    match = jnp.where(wanted == jnp.broadcast_to(ids, shape), 1.0, 0.0).astype(BF16)
    both = jnp.dot(match, split[...], preferred_element_type=F32)
    grad = both[:, :width] + both[:, width:]
    for k in range(rows // 128):
        at = slice(k * 128, (k + 1) * 128)
        line = pl.ds(n * (rows // 128) + k, 1)
        update, new_m, new_s, scale_m, scale_s = adam_parts(
            codes_m_ref[at, :],
            codes_s_ref[at, :],
            lanes_to_column(scale_m_ref[line, :], 128, 0),
            lanes_to_column(scale_s_ref[line, :], 128, 0),
            grad[at, :],
        )
        table_out[at, :] = table_ref[at, :] - update
        codes_m_out[at, :] = new_m
        codes_s_out[at, :] = new_s
        scale_m_out[line, :] = column_to_lanes(scale_m, 128)
        scale_s_out[line, :] = column_to_lanes(scale_s, 128)


def replica_kernel(table_ref, steps_ref, scale_ref, out_ref):
    piece = table_ref.shape[0] // scale_ref.shape[1]
    for k in range(scale_ref.shape[1]):
        at = slice(k * piece, (k + 1) * piece)
        scale = lanes_to_column(scale_ref[0, k : k + 1, :], piece, 0)
        out_ref[at, :] = table_ref[at, :] - steps_ref[0, at, :].astype(I32).astype(F32) * scale


def body(
    n_dp,
    n_row,
    bag_index,
    pooled_grad,
    touched_ids,
    owner_counts,
    cold_table,
    cold_moment_codes,
    cold_second_codes,
    cold_moment_scales,
    cold_second_scales,
    hot_table,
    hot_moment_codes,
    hot_second_codes,
    hot_moment_scales,
    hot_second_scales,
):
    samples, pool = bag_index.shape
    touch_rows = touched_ids.shape[1]
    width = pooled_grad.shape[1]
    hot_rows = hot_table.shape[0]
    own_rows = cold_table.shape[0]
    block = hot_rows // n_row
    slots = n_dp * CAP
    owners = n_dp * n_row

    counts = owner_counts[0]
    ends = jnp.cumsum(counts)
    spare = CAP - counts
    bag = bag_index.T
    padding = jnp.sum(
        jnp.where(ends[:, None, None] <= bag[None], spare[:, None, None], 0), axis=0
    )
    spread = bag + padding
    owner, place = spread // CAP, spread % CAP
    slot = (owner % n_row) * slots + (owner // n_row) * CAP + place
    code = jnp.where(bag < touch_rows, slot, bag - touch_rows + owners * CAP)
    packed = code[:, : samples // 2] | (code[:, samples // 2 :] << 16)
    lane = lax.broadcasted_iota(I32, (n_row, n_dp, CAP), 2)
    by_row = counts.reshape(n_dp, n_row).T
    starts = (ends - counts).reshape(n_dp, n_row).T
    position = jnp.where(lane < by_row[:, :, None], starts[:, :, None] + lane, -1).reshape(n_row, slots)
    spots = lax.iota(I32, touch_rows)
    slot_ids = jnp.sum(
        jnp.where(spots[:, None, None] == position[None], touched_ids[0][:, None, None] + 1, 0), axis=0
    ) - 1
    note = jnp.concatenate([packed, slot_ids], axis=1)

    chips = n_row // 2
    main_hops, other_hops = chips // 2, chips // 2 - 1
    flows = main_hops + 1 + other_hops
    vmem = pl.BlockSpec(memory_space=pltpu.VMEM)
    cold_in, ids_in, steps_q, steps_scale, new_m, new_s, lines = pl.pallas_call(
        functools.partial(exchange_kernel, n_dp, n_row),
        out_shape=(
            jax.ShapeDtypeStruct((n_dp, n_row, CAP, width), F32),
            jax.ShapeDtypeStruct((n_dp, n_row, slots), I32),
            jax.ShapeDtypeStruct((n_row, block, width), jnp.int16),
            jax.ShapeDtypeStruct((n_row, n_dp, 128), F32),
            jax.ShapeDtypeStruct((block, width), BF16),
            jax.ShapeDtypeStruct((block, width), BF16),
            jax.ShapeDtypeStruct((n_dp, 8, 128), F32),
        ),
        in_specs=[vmem] * 6,
        out_specs=(vmem,) * 7,
        scratch_shapes=[
            pltpu.VMEM((n_row, samples, width), BF16),
            pltpu.VMEM((n_row, pool, samples // 2 + slots), I32),
            pltpu.VMEM((block + slots, samples // 2), BF16),
            pltpu.VMEM((block, width), F32),
            pltpu.VMEM((n_row, slots, width), F32),
            pltpu.VMEM((n_row, slots), I32),
            pltpu.VMEM((n_dp, block // n_dp, width), F32),
            pltpu.VMEM((8, 128), F32),
            pltpu.SemaphoreType.DMA((6, 2 * flows)),
            pltpu.SemaphoreType.DMA((6, flows)),
            pltpu.SemaphoreType.DMA((6, 2 * flows)),
            pltpu.SemaphoreType.DMA((6, flows)),
            pltpu.SemaphoreType.DMA((14,)),
            pltpu.SemaphoreType.DMA((2,)),
        ],
        compiler_params=pltpu.CompilerParams(
            collective_id=0, has_side_effects=True, vmem_limit_bytes=48 * 1024 * 1024
        ),
    )(
        pooled_grad,
        note,
        hot_moment_codes,
        hot_second_codes,
        hot_moment_scales.reshape(-1, 128),
        hot_second_scales.reshape(-1, 128),
    )

    ids = lax.dynamic_slice_in_dim(ids_in, lax.axis_index("dp") * CAP, CAP, 2).reshape(1, -1)
    tile = own_rows // 4
    lines_of = own_rows // 128
    whole = lambda a, b: pl.BlockSpec((a, b), lambda n: (0, 0))
    rows = pl.BlockSpec((tile, width), lambda n: (n, 0))
    cold = pl.pallas_call(
        cold_kernel,
        grid=(own_rows // tile,),
        out_shape=(
            jax.ShapeDtypeStruct((own_rows, width), F32),
            jax.ShapeDtypeStruct((own_rows, width), BF16),
            jax.ShapeDtypeStruct((own_rows, width), BF16),
            jax.ShapeDtypeStruct((lines_of, 128), F32),
            jax.ShapeDtypeStruct((lines_of, 128), F32),
        ),
        in_specs=[
            whole(owners * CAP, width),
            whole(1, owners * CAP),
            rows,
            rows,
            rows,
            whole(lines_of, 128),
            whole(lines_of, 128),
        ],
        out_specs=(rows, rows, rows, whole(lines_of, 128), whole(lines_of, 128)),
        scratch_shapes=[pltpu.VMEM((owners * CAP, 2 * width), BF16)],
    )(
        cold_in.reshape(-1, width),
        ids,
        cold_table,
        cold_moment_codes,
        cold_second_codes,
        cold_moment_scales.reshape(-1, 128),
        cold_second_scales.reshape(-1, 128),
    )
    replica = pl.pallas_call(
        replica_kernel,
        grid=(n_row,),
        out_shape=jax.ShapeDtypeStruct((hot_rows, width), F32),
        in_specs=[
            pl.BlockSpec((block, width), lambda n: (n, 0)),
            pl.BlockSpec((1, block, width), lambda n: (n, 0, 0)),
            pl.BlockSpec((1, n_dp, 128), lambda n: (n, 0, 0)),
        ],
        out_specs=pl.BlockSpec((block, width), lambda n: (n, 0)),
    )(hot_table, steps_q, steps_scale)
    piece = block // n_dp
    return (
        cold[0],
        cold[1],
        cold[2],
        cold[3].reshape(-1),
        cold[4].reshape(-1),
        replica,
        new_m,
        new_s,
        lines[:, 0, :piece].reshape(-1),
        lines[:, 1, :piece].reshape(-1),
    )


def solution(mesh):
    both = P(("dp", "row"), None)
    line = P(("dp", "row"))
    return jax.shard_map(
        functools.partial(body, mesh.shape["dp"], mesh.shape["row"]),
        mesh=mesh,
        in_specs=(
            both,
            both,
            both,
            both,
            both,
            both,
            both,
            line,
            line,
            P(),
            P("row", None),
            P("row", None),
            P("row"),
            P("row"),
        ),
        out_specs=(
            both,
            both,
            both,
            line,
            line,
            P(),
            P("row", None),
            P("row", None),
            P("row"),
            P("row"),
        ),
        check_vma=False,
    )
```

time: 420 us -> 130 us (0.31)
  waiting for transfers between devices: 148 us -> 0 us
  Pallas kernels: 0 us -> 108 us
  other arithmetic: 101 us -> 9.08 us
  matrix products: 37.9 us -> 0 us
  local copies, waits for them, and re-layouts: 47 us -> 11 us
  starting transfers between devices: 33.9 us -> 0 us
  blocking collectives: 33.7 us -> 0 us
  between operations: 14.3 us -> 0.75 us
    pallas_call x0 -> x3, Pallas kernels: none -> 108 us  [the longest x1 87.5 us: body(): pl.pallas_call(functools.partial(exchange_kernel, n_dp, n_row), out_shape...]
    all_to_all x3 -> x0, waiting for transfers between devices: 76.3 us -> none  [the longest x2 67.8 us: one_exchange(): tiles = lax.all_to_all(tiles, axis, split_axis=0, concat_axis=0, tiled=True)]
    reduce_scatter x1 -> x0, waiting for transfers between devices: 71.7 us -> none  [body(): lax.psum_scatter(hot_grad, 'row', scatter_dimension=0, tiled=True)]
    reduce_sum x19 -> x2, other arithmetic: 66.1 us -> 5.03 us  [the longest x1 3.16 us: body(): jnp.sum(jnp.where(spots[:, None, None] == position[None], touched_ids[0][...]
    dot_general x18 -> x0, matrix products: 37.9 us -> none  [tally_block(): lax.dot_general(tally, pooled_grad, (((0,), (0,)), ((), ())), preferred_e...]
    all_to_all x3 -> x0, starting transfers between devices: 33.9 us -> none  [the longest x2 27.1 us: one_exchange(): tiles = lax.all_to_all(tiles, axis, split_axis=0, concat_axis=0, tiled=True)]
    all_gather x2 -> x0, blocking collectives: 33.7 us -> none  [the longest x1 16.9 us: sent_together(): whole = lax.all_gather(both, axis, axis=dim, tiled=True)]
    gather x3 -> x0, local copies, waits for them, and re-layouts: 15.3 us -> none  [the longest x2 8.68 us: body(): touched_ids[0][position]]
  transfers between devices with their start and end apart: 5 -> 0, of which waited for: 4 -> 0; matrix products, arithmetic and copies ran while one was open for 10% -> 0% of each run, Pallas kernels for 0% -> 0%
where the time goes in v1:
time: 130 us; the launch traced here: 129 us
  Pallas kernels  108 us (83%)
  local copies, waits for them, and re-layouts  11 us (8%)
  other arithmetic  9.08 us (7%)
    pallas_call x1, Pallas kernels, body(): pl.pallas_call(functools.partial(exchange_kernel, n_dp, n_row), out_shape...  87.5 us
    pallas_call x1, Pallas kernels, body(): pl.pallas_call(replica_kernel, grid=(n_row,), out_shape=jax.ShapeDtypeStr...  13.6 us
    unnamed x17, local copies, waits for them, and re-layouts  8.09 us
    pallas_call x1, Pallas kernels, body(): pl.pallas_call(cold_kernel, grid=(own_rows // tile,), out_shape=(jax.Shap...  6.99 us
    reduce_sum x1, other arithmetic, body(): jnp.sum(jnp.where(spots[:, None, None] == position[None], touched_ids[0][...  3.16 us

profile of v1, /device:TPU:1, one launch (start us, length us, event | category | flops | bytes accessed | tf_op | source)
XLA Modules:
  0.0 128.8 jit_solution(1561706270591328724)
XLA Ops:
  0.6 1.0 reduce-window.9
  1.6 0.1 slice.19
  1.7 0.1 slice_reduce_fusion.2
  1.9 0.1 broadcast.87
  1.9 0.1 reshape.141
  2.0 0.1 add_bitcast_fusion
  2.1 0.5 broadcast.104
  2.6 1.3 %broadcast_subtract_fusion = (s32[1,256]{1,0:T(1,128)S(1)}, s32[256]{0:T(256)S(1)}) fusion(s32[1,256]{1,0:T(1,128)} %param.17, s32[]{:T(128)} %broadcast.104), kind=kLoop, calls=%fused_computation.39 | loop fusion | flops 256 | bytes 3076 | tf_op jit(solution)/shard_map/sub | solution.py:489
  3.9 0.7 broadcast_add_fusion.1
  4.6 0.1 reshape.140
  4.7 0.1 reshape_squeeze.9
  4.8 0.1 subtract_bitcast_fusion
  4.9 0.1 iota.24
  5.0 1.9 %select_reduce_fusion.1 = s32[16,512]{1,0:T(8,128)S(1)} fusion(s32[256]{0:T(256)S(1)} %bitcast.26, s32[16,512]{1,0:T(8,128)} %bitcast.24, s32[256]{0:T(256)S(1)} %add_bitcast_fusion), kind=kLoop, calls=%fused_computation.2 | loop fusion | flops 6283264 | bytes 67584 | tf_op jit(solution)/shard_map/reduce_sum | solution.py:491
  6.9 0.8 fusion.3
  7.8 3.2 %select_reduce_fusion = s32[16,128]{1,0:T(8,128)S(1)} fusion(s32[1024]{0:T(1024)S(1)} %bitcast.28, s32[16,128]{1,0:T(8,128)S(1)} %add_select_fusion.4), kind=kLoop, calls=%fused_computation | loop fusion | flops 6289408 | bytes 20480 | tf_op jit(solution)/shard_map/reduce_sum | solution.py:504
  11.0 0.9 copy-done.1
  12.0 0.9 copy-done.2
  12.9 0.9 copy-done.3
  13.9 0.7 copy-done.5
  14.6 0.7 copy-done.6
  15.3 87.5 %shard_map.213 = (f32[16,16,8,256]{3,2,1,0:T(8,128)S(1)}, s32[16,16,128]{2,1,0:T(8,128)S(1)}, s16[16,512,256]{2,1,0:T(8,128)(2,1)}, f32[16,16,128]{2,1,0:T(8,128...) custom-call(bf16[512,256]{1,0:T(8,128)(2,1)S(1)} %copy-done.1, ...), custom_call_target="tpu_custom_call" | custom-call | tf_op jit(solution)/shard_map/pallas_call | solution.py:513
  102.8 1.3 %copy-done = f32[16,16,8,256]{3,2,1,0:T(8,128)} copy-done((f32[16,16,8,256]{3,2,1,0:T(8,128)}, f32[16,16,8,256]{3,2,1,0:T(8,128)S(1)}, u32[]{:S(2)}) %copy-start) | copy-done | bytes 2097176
  104.1 0.7 copy-done.4
  104.8 0.7 reshape_squeeze.11
  105.4 0.7 reshape_squeeze.10
  106.1 0.1 constant_dynamic-slice_fusion
  106.2 0.7 reshape.145.ids_ref
  106.9 7.0 %shard_map.214 = (f32[1024,256]{1,0:T(8,128)}, bf16[1024,256]{1,0:T(8,128)(2,1)}, bf16[1024,256]{1,0:T(8,128)(2,1)}, f32[8,128]{1,0:T(8,128)}, f32[8,128]{1,0:T(8,128)}) custom-call(f32[2048,256]{1,0:T(8,128)} %bitcast.21, s32[1,2048]{1,0:T(1,128)} %reshape.145.ids_ref, f32[1024,256]{1,0:T(8,128)} %table_ref.2, bf16[1024,256]{1,0:T(8,128)(2,1)} %codes_m_ref.3, ...), custom_call_target="tpu_custom_call" | custom-call | tf_op jit(solution)/shard_map/pallas_call | solution.py:559
  113.9 13.6 %shard_map.215 = f32[8192,256]{1,0:T(8,128)} custom-call(f32[8192,256]{1,0:T(8,128)} %table_ref.3, s16[16,512,256]{2,1,0:T(8,128)(2,1)} %get-tuple-element.29.steps_ref, f32[16,16,128]{2,1,0:T(8,128)} %copy-done.4), custom_call_target="tpu_custom_call" | custom-call | tf_op jit(solution)/shard_map/pallas_call | solution.py:589
  127.4 0.7 copy.32
  128.1 0.7 copy.33
  (18 shorter events, 0.3 us)
Async XLA Ops:
  11.0 1.0 copy-start.1
  12.0 0.9 copy-start.2
  12.9 0.9 copy-start.3
  13.9 0.7 copy-start.5
  14.6 0.7 copy-start.6
  102.7 1.3 %copy-start = (f32[16,16,8,256]{3,2,1,0:T(8,128)}, f32[16,16,8,256]{3,2,1,0:T(8,128)S(1)}, u32[]{:S(2)}) copy-start(f32[16,16,8,256]{3,2,1,0:T(8,128)S(1)} %get-tuple-element.22) | copy-start | bytes 6291460
  104.1 0.7 copy-start.4

commit v2 on v1

--- a/solution.py
+++ b/solution.py
@@ -47,6 +47,43 @@
     shape = (column.shape[0], lanes)
     at = lax.broadcasted_iota(I32, shape, 1) == lax.broadcasted_iota(I32, shape, 0)
     return jnp.sum(jnp.where(at, jnp.broadcast_to(column, shape), 0.0), axis=0, keepdims=True)
+
+
+def note_kernel(n_dp, n_row, counts_ref, touched_ref, bag, note_ref):
+    slots = n_dp * CAP
+    half = bag.shape[1] // 2
+    lane = lax.broadcasted_iota(I32, (n_row, slots), 1)
+    owner_of = (lane // CAP) * n_row + lax.broadcasted_iota(I32, (n_row, slots), 0)
+    entries = bag[...]
+
+    def owner_step(o, carry):
+        padding, start_of, count_of, start = carry
+        held = counts_ref[0, o]
+        end = start + held
+        here = owner_of == o
+        return (
+            padding + jnp.where(entries >= end, CAP - held, 0),
+            jnp.where(here, start, start_of),
+            jnp.where(here, held, count_of),
+            end,
+        )
+
+    none = jnp.zeros((n_row, slots), I32)
+    padding, start_of, count_of, _ = lax.fori_loop(
+        0, n_dp * n_row, owner_step, (jnp.zeros_like(entries), none, none, jnp.int32(0)), unroll=8
+    )
+    spread = entries + padding
+    owner, place = spread // CAP, spread & (CAP - 1)
+    slot = (owner & (n_row - 1)) * slots + (owner // n_row) * CAP + place
+    touch_rows = touched_ref.shape[1]
+    code = jnp.where(entries < touch_rows, slot, entries - touch_rows + n_row * slots)
+    note_ref[:, :half] = code[:, :half] | lax.shift_left(code[:, half:], 16)
+    position = jnp.where((lane & (CAP - 1)) < count_of, start_of + (lane & (CAP - 1)), -1)
+
+    def touched_step(t, found):
+        return jnp.where(position == t, touched_ref[0, t], found)
+
+    note_ref[:, half:] = lax.fori_loop(0, touch_rows, touched_step, none - 1, unroll=16)
 
 
 def exchange_kernel(
@@ -450,11 +487,15 @@
 
 
 def replica_kernel(table_ref, steps_ref, scale_ref, out_ref):
-    piece = table_ref.shape[0] // scale_ref.shape[1]
-    for k in range(scale_ref.shape[1]):
-        at = slice(k * piece, (k + 1) * piece)
-        scale = lanes_to_column(scale_ref[0, k : k + 1, :], piece, 0)
-        out_ref[at, :] = table_ref[at, :] - steps_ref[0, at, :].astype(I32).astype(F32) * scale
+    blocks, pieces = scale_ref.shape[:2]
+    block = steps_ref.shape[1]
+    piece = block // pieces
+    for n in range(blocks):
+        for k in range(pieces):
+            at = slice(n * block + k * piece, n * block + (k + 1) * piece)
+            scale = lanes_to_column(scale_ref[n, k : k + 1, :], piece, 0)
+            moved = steps_ref[n, k * piece : (k + 1) * piece, :].astype(I32).astype(F32)
+            out_ref[at, :] = table_ref[at, :] - moved * scale
 
 
 def body(
@@ -476,7 +517,6 @@
     hot_second_scales,
 ):
     samples, pool = bag_index.shape
-    touch_rows = touched_ids.shape[1]
     width = pooled_grad.shape[1]
     hot_rows = hot_table.shape[0]
     own_rows = cold_table.shape[0]
@@ -484,32 +524,19 @@
     slots = n_dp * CAP
     owners = n_dp * n_row
 
-    counts = owner_counts[0]
-    ends = jnp.cumsum(counts)
-    spare = CAP - counts
-    bag = bag_index.T
-    padding = jnp.sum(
-        jnp.where(ends[:, None, None] <= bag[None], spare[:, None, None], 0), axis=0
-    )
-    spread = bag + padding
-    owner, place = spread // CAP, spread % CAP
-    slot = (owner % n_row) * slots + (owner // n_row) * CAP + place
-    code = jnp.where(bag < touch_rows, slot, bag - touch_rows + owners * CAP)
-    packed = code[:, : samples // 2] | (code[:, samples // 2 :] << 16)
-    lane = lax.broadcasted_iota(I32, (n_row, n_dp, CAP), 2)
-    by_row = counts.reshape(n_dp, n_row).T
-    starts = (ends - counts).reshape(n_dp, n_row).T
-    position = jnp.where(lane < by_row[:, :, None], starts[:, :, None] + lane, -1).reshape(n_row, slots)
-    spots = lax.iota(I32, touch_rows)
-    slot_ids = jnp.sum(
-        jnp.where(spots[:, None, None] == position[None], touched_ids[0][:, None, None] + 1, 0), axis=0
-    ) - 1
-    note = jnp.concatenate([packed, slot_ids], axis=1)
+    vmem = pl.BlockSpec(memory_space=pltpu.VMEM)
+    smem = pl.BlockSpec(memory_space=pltpu.SMEM)
+    note = pl.pallas_call(
+        functools.partial(note_kernel, n_dp, n_row),
+        out_shape=jax.ShapeDtypeStruct((pool, samples // 2 + slots), I32),
+        in_specs=[smem, smem, vmem],
+        out_specs=vmem,
+        compiler_params=pltpu.CompilerParams(vmem_limit_bytes=63 * 1024 * 1024),
+    )(owner_counts, touched_ids, bag_index.T)
 
     chips = n_row // 2
     main_hops, other_hops = chips // 2, chips // 2 - 1
     flows = main_hops + 1 + other_hops
-    vmem = pl.BlockSpec(memory_space=pltpu.VMEM)
     cold_in, ids_in, steps_q, steps_scale, new_m, new_s, lines = pl.pallas_call(
         functools.partial(exchange_kernel, n_dp, n_row),
         out_shape=(
@@ -540,7 +567,7 @@
             pltpu.SemaphoreType.DMA((2,)),
         ],
         compiler_params=pltpu.CompilerParams(
-            collective_id=0, has_side_effects=True, vmem_limit_bytes=48 * 1024 * 1024
+            collective_id=0, has_side_effects=True, vmem_limit_bytes=63 * 1024 * 1024
         ),
     )(
         pooled_grad,
@@ -588,14 +615,14 @@
     )
     replica = pl.pallas_call(
         replica_kernel,
-        grid=(n_row,),
+        grid=(n_row // 4,),
         out_shape=jax.ShapeDtypeStruct((hot_rows, width), F32),
         in_specs=[
-            pl.BlockSpec((block, width), lambda n: (n, 0)),
-            pl.BlockSpec((1, block, width), lambda n: (n, 0, 0)),
-            pl.BlockSpec((1, n_dp, 128), lambda n: (n, 0, 0)),
+            pl.BlockSpec((4 * block, width), lambda n: (n, 0)),
+            pl.BlockSpec((4, block, width), lambda n: (n, 0, 0)),
+            pl.BlockSpec((4, n_dp, 128), lambda n: (n, 0, 0)),
         ],
-        out_specs=pl.BlockSpec((block, width), lambda n: (n, 0)),
+        out_specs=pl.BlockSpec((4 * block, width), lambda n: (n, 0)),
     )(hot_table, steps_q, steps_scale)
     piece = block // n_dp
     return (

time: 130 us -> 115 us (0.88)
  other arithmetic: 9.08 us -> 0 us
  local copies, waits for them, and re-layouts: 11 us -> 5.4 us
    unnamed x17 -> x6, local copies, waits for them, and re-layouts: 8.09 us -> 1.41 us
    reduce_sum x2 -> x0, other arithmetic: 5.03 us -> none  [the longest x1 3.16 us: body(): jnp.sum(jnp.where(spots[:, None, None] == position[None], touched_ids[0][...]
    pallas_call x1, Pallas kernels: 87.5 us -> 89.5 us  [body(): pl.pallas_call(functools.partial(exchange_kernel, n_dp, n_row), out_shape...]
    sub x2 -> x0, other arithmetic: 1.34 us -> none  [the longest x1 1.34 us: body(): spare = CAP - counts]
    pallas_call x1 -> x2, Pallas kernels: 13.6 us -> 12.2 us  [the longest x1 8.48 us: body(): pl.pallas_call(replica_kernel, grid=(n_row // 4,), out_shape=jax.ShapeDty...]
where the time goes in v2:
time: 115 us
  Pallas kernels  109 us (95%)
  local copies, waits for them, and re-layouts  5.4 us (5%)
    pallas_call x1, Pallas kernels, body(): pl.pallas_call(functools.partial(exchange_kernel, n_dp, n_row), out_shape...  89.5 us
    pallas_call x1, Pallas kernels, body(): pl.pallas_call(replica_kernel, grid=(n_row // 4,), out_shape=jax.ShapeDty...  8.48 us
    pallas_call x1, Pallas kernels, body(): pl.pallas_call(cold_kernel, grid=(own_rows // tile,), out_shape=(jax.Shap...  6.99 us
    pallas_call x1, Pallas kernels, body(): pl.pallas_call(functools.partial(note_kernel, n_dp, n_row), out_shape=jax...  3.75 us

profile of v2, /device:TPU:1, one launch (start us, length us, event | category | flops | bytes accessed | tf_op | source)
XLA Modules:
  0.0 114.8 jit_solution(16182657921850178308)
XLA Ops:
  0.6 3.7 %shard_map.213.note_ref = s32[16,384]{1,0:T(8,128)} custom-call(s32[1,256]{1,0:T(1,128)} %counts_ref.1, s32[1,1024]{1,0:T(1,128)} %touched_ref.1, s32[16,512]{1,0:T(8,128)} %bitcast.9), custom_call_target="tpu_custom_call" | custom-call | tf_op jit(solution)/shard_map/pallas_call | solution.py:529
  4.4 89.5 %shard_map.214 = (f32[16,16,8,256]{3,2,1,0:T(8,128)}, s32[16,16,128]{2,1,0:T(8,128)}, s16[16,512,256]{2,1,0:T(8,128)(2,1)}, f32[16,16,128]{2,1,0:T(8,128)}, bf16...) custom-call(bf16[512,256]{1,0:T(8,128)(2,1)} %pool_ref.1, s32[16,384]{1,0:T(8,128)} %shard_map.213.note_ref, ...), custom_call_target="tpu_custom_call" | custom-call | tf_op jit(solution)/shard_map/pallas_call | solution.py:540
  93.9 1.0 slice_reduce_fusion
  94.9 0.7 reshape_squeeze.7
  95.5 0.7 reshape_squeeze.6
  96.2 1.0 constant_dynamic-slice_fusion
  97.2 0.7 reshape.47.ids_ref
  97.9 7.0 %shard_map.215 = (f32[1024,256]{1,0:T(8,128)}, bf16[1024,256]{1,0:T(8,128)(2,1)}, bf16[1024,256]{1,0:T(8,128)(2,1)}, f32[8,128]{1,0:T(8,128)}, f32[8,128]{1,0:T(8,128)}) custom-call(f32[2048,256]{1,0:T(8,128)} %bitcast.8, s32[1,2048]{1,0:T(1,128)} %reshape.47.ids_ref, f32[1024,256]{1,0:T(8,128)} %table_ref.2, bf16[1024,256]{1,0:T(8,128)(2,1)} %codes_m_ref.3, ...), custom_call_target="tpu_custom_call" | custom-call | tf_op jit(solution)/shard_map/pallas_call | solution.py:586
  104.9 0.0 copy-start.1
  104.9 0.0 copy-start
  104.9 8.5 %shard_map.216 = f32[8192,256]{1,0:T(8,128)} custom-call(f32[8192,256]{1,0:T(8,128)} %table_ref.3, s16[16,512,256]{2,1,0:T(8,128)(2,1)} %get-tuple-element.29.steps_ref, f32[16,16,128]{2,1,0:T(8,128)} %get-tuple-element.30.scale_ref), custom_call_target="tpu_custom_call" | custom-call | tf_op jit(solution)/shard_map/pallas_call | solution.py:616
  113.4 0.0 copy-done.1
  113.4 0.7 copy.26
  114.1 0.0 copy-done
  114.1 0.7 copy.27
Async XLA Ops:
  104.9 8.5 %copy-start.1 = (bf16[512,256]{1,0:T(8,128)(2,1)S(1)}, bf16[512,256]{1,0:T(8,128)(2,1)}, u32[]{:S(2)}) copy-start(bf16[512,256]{1,0:T(8,128)(2,1)} %get-tuple-element.52) | copy-start | bytes 786436
  104.9 9.2 %copy-start = (bf16[512,256]{1,0:T(8,128)(2,1)S(1)}, bf16[512,256]{1,0:T(8,128)(2,1)}, u32[]{:S(2)}) copy-start(bf16[512,256]{1,0:T(8,128)(2,1)} %get-tuple-element.53) | copy-start | bytes 786436

commit v3 on v2

--- a/solution.py
+++ b/solution.py
@@ -441,6 +441,7 @@
 def cold_kernel(
     values_ref,
     ids_ref,
+    lines_ref,
     table_ref,
     codes_m_ref,
     codes_s_ref,
@@ -451,7 +452,10 @@
     codes_s_out,
     scale_m_out,
     scale_s_out,
+    hot_scale_m_out,
+    hot_scale_s_out,
     split,
+    ids_line,
 ):
     n = pl.program_id(0)
     rows, width = table_ref.shape
@@ -462,8 +466,31 @@
         top = value.astype(BF16)
         split[:, :width] = top
         split[:, width:] = (value - top.astype(F32)).astype(BF16)
-
-    ids = ids_ref[...]
+        d = lax.axis_index("dp")
+        senders, _, slots = ids_ref.shape
+        for k in range(senders):
+            x = ids_ref[k]
+            lane = lax.broadcasted_iota(I32, x.shape, 1)
+            x = jnp.where(lane // CAP == d, x, 0)
+            shift = CAP
+            while shift < slots:
+                x = x + pltpu.roll(x, shift, 1)
+                shift *= 2
+            own = lane // CAP == lax.broadcasted_iota(I32, x.shape, 0)
+            ids_line[0:1, k * slots : (k + 1) * slots] = jnp.sum(
+                jnp.where(own, x, 0), axis=0, keepdims=True
+            )
+        lines = hot_scale_m_out.shape[0]
+        per_line = senders // lines
+        piece = 128 // per_line
+        for ref, out in ((0, hot_scale_m_out), (1, hot_scale_s_out)):
+            for k in range(lines):
+                line = lines_ref[k * per_line, ref : ref + 1, :]
+                for i in range(1, per_line):
+                    line = line + pltpu.roll(lines_ref[k * per_line + i, ref : ref + 1, :], i * piece, 1)
+                out[k : k + 1, :] = line
+
+    ids = ids_line[...]
     shape = (rows, ids.shape[1])
     wanted = lax.broadcasted_iota(I32, shape, 0) + n * rows
     match = jnp.where(wanted == jnp.broadcast_to(ids, shape), 1.0, 0.0).astype(BF16)
@@ -578,7 +605,8 @@
         hot_second_scales.reshape(-1, 128),
     )
 
-    ids = lax.dynamic_slice_in_dim(ids_in, lax.axis_index("dp") * CAP, CAP, 2).reshape(1, -1)
+    hot_lines = block // 128
+    whole3 = lambda a: pl.BlockSpec(a.shape, lambda n: (0, 0, 0))
     tile = own_rows // 4
     lines_of = own_rows // 128
     whole = lambda a, b: pl.BlockSpec((a, b), lambda n: (0, 0))
@@ -592,21 +620,36 @@
             jax.ShapeDtypeStruct((own_rows, width), BF16),
             jax.ShapeDtypeStruct((lines_of, 128), F32),
             jax.ShapeDtypeStruct((lines_of, 128), F32),
+            jax.ShapeDtypeStruct((hot_lines, 128), F32),
+            jax.ShapeDtypeStruct((hot_lines, 128), F32),
         ),
         in_specs=[
             whole(owners * CAP, width),
-            whole(1, owners * CAP),
+            whole3(ids_in),
+            whole3(lines),
             rows,
             rows,
             rows,
             whole(lines_of, 128),
             whole(lines_of, 128),
         ],
-        out_specs=(rows, rows, rows, whole(lines_of, 128), whole(lines_of, 128)),
-        scratch_shapes=[pltpu.VMEM((owners * CAP, 2 * width), BF16)],
+        out_specs=(
+            rows,
+            rows,
+            rows,
+            whole(lines_of, 128),
+            whole(lines_of, 128),
+            whole(hot_lines, 128),
+            whole(hot_lines, 128),
+        ),
+        scratch_shapes=[
+            pltpu.VMEM((owners * CAP, 2 * width), BF16),
+            pltpu.VMEM((1, owners * CAP), I32),
+        ],
     )(
         cold_in.reshape(-1, width),
-        ids,
+        ids_in,
+        lines,
         cold_table,
         cold_moment_codes,
         cold_second_codes,
@@ -624,7 +667,6 @@
         ],
         out_specs=pl.BlockSpec((4 * block, width), lambda n: (n, 0)),
     )(hot_table, steps_q, steps_scale)
-    piece = block // n_dp
     return (
         cold[0],
         cold[1],
@@ -634,8 +676,8 @@
         replica,
         new_m,
         new_s,
-        lines[:, 0, :piece].reshape(-1),
-        lines[:, 1, :piece].reshape(-1),
+        cold[5].reshape(-1),
+        cold[6].reshape(-1),
     )
 
 

time: 115 us -> 112 us (0.974)
  local copies, waits for them, and re-layouts: 5.4 us -> 1.41 us
    another operation x2 -> x0, local copies, waits for them, and re-layouts: 1.31 us -> none  [the longest x1 0.66 us: body(): lines[:, 1, :piece].reshape(-1)]
where the time goes in v3:
time: 112 us; the launch traced here: 111 us
  Pallas kernels  109 us (97%)
  local copies, waits for them, and re-layouts  1.41 us (1%)
    pallas_call x1, Pallas kernels, body(): pl.pallas_call(functools.partial(exchange_kernel, n_dp, n_row), out_shape...  89.5 us
    pallas_call x1, Pallas kernels, body(): pl.pallas_call(replica_kernel, grid=(n_row // 4,), out_shape=jax.ShapeDty...  8.48 us
    pallas_call x1, Pallas kernels, body(): pl.pallas_call(cold_kernel, grid=(own_rows // tile,), out_shape=(jax.Shap...  7.62 us
    pallas_call x1, Pallas kernels, body(): pl.pallas_call(functools.partial(note_kernel, n_dp, n_row), out_shape=jax...  3.75 us

profile of v3, /device:TPU:1, one launch (start us, length us, event | category | flops | bytes accessed | tf_op | source)
XLA Modules:
  0.0 111.5 jit_solution(4088851752215625573)
XLA Ops:
  0.6 3.7 %shard_map.213.note_ref = s32[16,384]{1,0:T(8,128)} custom-call(s32[1,256]{1,0:T(1,128)} %counts_ref.1, s32[1,1024]{1,0:T(1,128)} %touched_ref.1, s32[16,512]{1,0:T(8,128)} %bitcast.11), custom_call_target="tpu_custom_call" | custom-call | tf_op jit(solution)/shard_map/pallas_call | solution.py:556
  4.4 89.5 %shard_map.214 = (f32[16,16,8,256]{3,2,1,0:T(8,128)}, s32[16,16,128]{2,1,0:T(8,128)}, s16[16,512,256]{2,1,0:T(8,128)(2,1)}, f32[16,16,128]{2,1,0:T(8,128)}, bf16...) custom-call(bf16[512,256]{1,0:T(8,128)(2,1)} %pool_ref.1, s32[16,384]{1,0:T(8,128)} %shard_map.213.note_ref, ...), custom_call_target="tpu_custom_call" | custom-call | tf_op jit(solution)/shard_map/pallas_call | solution.py:567
  93.9 7.6 %shard_map.215 = (f32[1024,256]{1,0:T(8,128)}, bf16[1024,256]{1,0:T(8,128)(2,1)}, bf16[1024,256]{1,0:T(8,128)(2,1)}, f32[8,128]{1,0:T(8,128)}, f32[8,128]{1,0:T(...) custom-call(f32[2048,256]{1,0:T(8,128)} %bitcast.10, s32[16,16,128]{2,1,0:T(8,128)} %get-tuple-element.25.ids_ref, ...), custom_call_target="tpu_custom_call" | custom-call | tf_op jit(solution)/shard_map/pallas_call | solution.py:614
  101.6 0.0 copy-start.1
  101.6 0.0 copy-start
  101.6 8.5 %shard_map.216 = f32[8192,256]{1,0:T(8,128)} custom-call(f32[8192,256]{1,0:T(8,128)} %table_ref.3, s16[16,512,256]{2,1,0:T(8,128)(2,1)} %get-tuple-element.32.steps_ref, f32[16,16,128]{2,1,0:T(8,128)} %get-tuple-element.33.scale_ref), custom_call_target="tpu_custom_call" | custom-call | tf_op jit(solution)/shard_map/pallas_call | solution.py:659
  110.1 0.0 copy-done.1
  110.1 0.7 copy.26
  110.8 0.0 copy-done
  110.8 0.7 copy.27
Async XLA Ops:
  101.6 8.5 %copy-start.1 = (bf16[512,256]{1,0:T(8,128)(2,1)S(1)}, bf16[512,256]{1,0:T(8,128)(2,1)}, u32[]{:S(2)}) copy-start(bf16[512,256]{1,0:T(8,128)(2,1)} %get-tuple-element.54) | copy-start | bytes 786436
  101.6 9.2 %copy-start = (bf16[512,256]{1,0:T(8,128)(2,1)S(1)}, bf16[512,256]{1,0:T(8,128)(2,1)}, u32[]{:S(2)}) copy-start(bf16[512,256]{1,0:T(8,128)(2,1)} %get-tuple-element.55) | copy-start | bytes 786436
